TPU v7x, 256 devices: a whole 4x4x8 slice. The times are simulated.
256 devices in a mesh: items: 4 (over x), users: 64 (over z, y, core).
Axes of the slice: x: 4, y: 4, z: 8, core: 2. Of those that a mesh axis runs over, the one named last changes fastest.
Arguments:
- capsules: bfloat16 [4096, 8, 128], P('users'), may hold values from -6 to 6
- bank: bfloat16 [262144, 128], P(('items', 'users')), may hold values from -0.5 to 0.5
Outputs:
- relative: float32 [4096, 256], P('users', 'items')
- peak: float32 [4096], P('users')
All inputs are finite; a program needn't handle non-finite values.
Results may differ from a plain program's by a relative error of at most 0.0003.
Values may be sent and summed in bfloat16 or wider, within the bound.
A program may use at most 64 MiB of HBM per device.

v0:
```python
import jax
import jax.numpy as jnp
from jax import lax
from jax.sharding import PartitionSpec as P

BLOCK = 1024


def sent_to_all(value, axis):
    length = lax.axis_size(axis)
    return lax.all_to_all(
        jnp.broadcast_to(value[None], (length, *value.shape)), axis, 0, 0, tiled=True
    )


def of_everyone(value, axis):
    return sent_to_all(value, axis).max(axis=0)


def block_peaks(caps, rows):
    users_here = caps.shape[0]
    flat = caps.reshape(users_here * caps.shape[1], caps.shape[2])
    count = rows.shape[0] // BLOCK
    blocks = rows.reshape(count, BLOCK, rows.shape[1])

    def one_block(item_rows):
        score = lax.dot_general(
            flat, item_rows, (((1,), (1,)), ((), ())), preferred_element_type=jnp.float32
        )
        return jnp.max(score.reshape(users_here, -1), axis=1)

    return lax.map(one_block, blocks).T


def per_device(capsules, bank):
    everyone = lax.all_gather(capsules, "users", axis=0, tiled=True)
    own_block = block_peaks(everyone, bank)
    table = lax.all_to_all(own_block, "users", split_axis=0, concat_axis=1, tiled=True)
    peak = of_everyone(jnp.max(table, axis=1), "items")
    return (table - peak[:, None], peak)


def solution(mesh):
    return jax.shard_map(
        per_device,
        mesh=mesh,
        in_specs=(P("users", None, None), P(("items", "users"), None)),
        out_specs=(P("users", "items"), P("users")),
        check_vma=False,
    )
```

profile of v0, /device:TPU:1, one launch (start us, length us, event | category | flops | bytes accessed | tf_op | source)
XLA Modules:
  0.0 152.0 jit_solution(13896020500113062206)
XLA Ops:
  7.2 0.0 copy-start
  7.2 0.0 all-gather.2.cloned.1.call-start
  7.2 0.7 all-gather.2.cloned.1.call-update
  7.9 90.1 %all-gather.2.cloned.1.call-done = bf16[4096,8,128]{2,1,0:T(8,128)(2,1)} async-done(((bf16[64,8,128]{2,1,0:T(8,128)(2,1)}), bf16[4096,8,128]{2,1,0:T(8,128)(2,1)}) %all-gather.2.cloned.1.call-update) | async-done | bytes 8388624 | tf_op jit(solution)/shard_map/all_gather | solution.py:36
  98.0 0.0 copy-done
  98.0 21.6 %convolution_reduce_fusion = f32[32768]{0:T(1024)S(1)} fusion(bf16[1024,128]{1,0:T(8,128)(2,1)S(1)} %copy-done, bf16[4096,8,128]{2,1,0:T(8,128)(2,1)} %all-gather.2.cloned.1.call-done), kind=kOutput, calls=%fused_computation | convolution fusion | flops 8623456256 | bytes 8781824 | tf_op jit(solution)/shard_map/while/body/eval_jaxpr/dot_general | solution.py:27
  119.6 1.1 reduce_max.36
  120.7 0.6 reduce_max.37
  121.3 0.1 all_to_all.18
  121.4 15.0 %all_to_all.25 = f32[64,64,1]{1,2,0:T(1,128)S(1)} all-to-all(f32[64,64,1]{1,2,0:T(1,128)S(1)} %bitcast.10), channel_id=1, replica_groups=mesh['items'=4,'users'=64] {'users'}, dimensions={0} | all-to-all | bytes 32768 | tf_op jit(solution)/shard_map/all_to_all | solution.py:38
  136.4 0.1 reduce_max.38
  136.5 7.9 %all_to_all.26 = f32[4,1,64]{2,1,0:T(1,128)S(1)} all-to-all(f32[4,1,64]{2,1,0:T(1,128)S(1)} %broadcast_in_dim.5), channel_id=1, replica_groups=mesh['items'=4,'users'=64] {'items'}, dimensions={0} | all-to-all | bytes 2048 | tf_op jit(solution)/shard_map/all_to_all | solution.py:11
  144.4 0.0 copy-start.1
  144.4 0.7 copy.11
  145.1 0.0 copy-done.1
  (3 shorter events, 0.0 us)
Async XLA Ops:
  7.2 90.8 %copy-start = (bf16[1024,128]{1,0:T(8,128)(2,1)S(1)}, bf16[1024,128]{1,0:T(8,128)(2,1)}, u32[]{:S(2)}) copy-start(bf16[1024,128]{1,0:T(8,128)(2,1)} %param.3) | copy-start | bytes 786436
  7.2 90.8 %all-gather.2.cloned.1.call-start = ((), (), s32[]{:S(2)}) async-start(), calls=%async_computation.2 | async-start | bytes 8519680 | tf_op jit(solution)/shard_map/all_gather | solution.py:36
  144.4 0.7 copy-start.1
Sparse Core Ops, SparseCore 0:
  10.8 87.1 all-gather.1
where the time goes:
time: 152 us
  waiting for transfers between devices  90.8 us (60%)
  blocking collectives  22.9 us (15%)
  matrix products  21.6 us (14%)
  between operations  14.1 us (9%)
  local copies, waits for them, and re-layouts  1.92 us (1%)
    all_gather x1, waiting for transfers between devices, per_device(): everyone = lax.all_gather(capsules, 'users', axis=0, tiled=True)  90.1 us
    dot_general x1, matrix products, one_block(): lax.dot_general(flat, item_rows, (((1,), (1,)), ((), ())), preferred_elem...  21.6 us
    all_to_all x1, blocking collectives, per_device(): lax.all_to_all(own_block, 'users', split_axis=0, concat_axis=1, tiled=True)  15 us
    all_to_all x1, blocking collectives, sent_to_all(): lax.all_to_all(jnp.broadcast_to(value[None], (length, *value.shape)), axi...  7.9 us
  transfers between devices with their start and end apart: 1, of which 1 were waited for; matrix products, arithmetic and copies ran while one was open for 0% of the time, Pallas kernels for 0%

commit v1 on v0

v1 whole, which is shorter than its diff:
```python
import jax
import jax.numpy as jnp
from jax import lax
from jax.experimental import pallas as pl
from jax.experimental.pallas import tpu as pltpu
from jax.sharding import PartitionSpec as P

K = 8
E = 128
BLOCK = 1024
USERS = 64
NX, NZ, NY = 4, 8, 4
COLS = USERS * K
TILE = COLS // 2
HALF = BLOCK // 2
ROWS = 256
MESH = pl.DeviceIdType.MESH

DZ = (0, -1, -2, -3, 1, 2, 3, 4)
DY = (0, -1, 1, 2)


def units_of(groups, blocks):
    return [("u", g, b, h) for g in groups for b, h in blocks]


def full(*slots):
    return [(b, h) for b in slots for h in (0, 1)]


def half(h, *slots):
    return [(b, h) for b in slots]


def wait_c(*pieces):
    return [("c", s, t) for s, t in pieces]


def wait_b(*pieces):
    return [("b", s, h) for s, h in pieces]


def program():
    order = []
    order += units_of([0], full(0))
    order += wait_b((4, 0), (4, 1))
    order += units_of([0], full(4))
    order += wait_c((1, 0), (4, 1), (1, 1))
    order += units_of([1], full(0, 4))
    order += wait_c((4, 0)) + wait_b((1, 0), (2, 0))
    order += units_of([4], full(0, 4))
    order += units_of([0, 1, 4], half(0, 1, 2))
    order += wait_b((5, 0), (6, 0)) + wait_c((2, 0), (5, 1))
    order += units_of([0, 1, 4], half(0, 5, 6))
    order += wait_c((2, 1), (5, 0)) + wait_b((1, 1), (2, 1))
    order += units_of([2, 5], full(0, 4) + half(0, 1, 2, 5, 6))
    order += wait_b((5, 1), (6, 1)) + wait_c((3, 0), (6, 1))
    order += units_of([2, 5], half(1, 1, 2, 5, 6))
    order += wait_c((3, 1), (6, 0)) + wait_b((3, 0), (3, 1))
    order += units_of([3, 6], full(0, 4, 1, 2, 5, 6))
    order += wait_b((7, 0), (7, 1)) + wait_c((7, 0), (7, 1)) + [("ready1",)]
    order += units_of([7], full(0, 4, 1, 2))
    order += [("ready2",)]
    order += units_of([7], full(5, 6))
    order += [("ready3",)]
    order += units_of([7, 3, 6, 2, 5], full(3, 7))
    order += units_of([1, 4, 0], half(1, 1, 2, 5, 6) + full(3, 7))
    assert len({o for o in order if o[0] == "u"}) == 128
    return order


def widened(value):
    return jnp.concatenate([value, jnp.zeros_like(value)], axis=1)


def kernel(
    caps_hbm, bank_hbm, out_ref, peak_ref,
    caps, bank, peaks, rows, tiles, table, turned,
    local_sem, cap_sem, bank_sem, tile_sem, cap_send, bank_send, tile_send, ready_a, ready_b,
):
    x = lax.axis_index("items")
    u = lax.axis_index("users")
    z = lax.div(u, 2 * NY)
    y = lax.rem(lax.div(u, 2), NY)
    core = lax.rem(u, 2)
    xs = [lax.rem(x + dx, NX) for dx in range(NX)]
    ys = [lax.rem(y + dy, NY) for dy in range(NY)]
    zs = [lax.rem(z + dz, NZ) for dz in range(NZ)]
    here = x * NZ + z
    users_at = {}
    for dz in range(NZ):
        users_at[dz, 0, 0] = (zs[dz] * NY + y) * 2 + core
    for dy in range(1, NY):
        users_at[0, dy, 0] = (z * NY + ys[dy]) * 2 + core
    users_at[0, 0, 1] = (z * NY + y) * 2 + 1 - core
    row_of = [2 * ys[DY[b % 4] % NY] + (core if b < 4 else 1 - core) for b in range(8)]

    def device(dx=0, dz=0, dy=0, flip=0):
        return {"items": xs[dx % NX], "users": users_at[dz % NZ, dy % NY, flip]}

    def cap_part(slot, t):
        return caps.at[slot, pl.ds(t * TILE, TILE), :]

    def bank_part(slot, h):
        return bank.at[slot, pl.ds(h * HALF, HALF), :]

    sent = []

    def send(src, dst, send_sem, recv_sem, to):
        copy = pltpu.make_async_remote_copy(
            src_ref=src, dst_ref=dst, send_sem=send_sem, recv_sem=recv_sem, device_id=to, device_id_type=MESH
        )
        copy.start()
        sent.append(copy)

    counts = {"c": 0, "b": 0, "t": 0}

    def send_cap(slot, t, to_slot, dz):
        n = counts["c"]
        counts["c"] += 1
        send(cap_part(slot, t), cap_part(to_slot, t), cap_send.at[n], cap_sem.at[to_slot, t], device(dz=dz))

    def send_bank(slot, h, to_slot, **to):
        n = counts["b"]
        counts["b"] += 1
        send(bank_part(slot, h), bank_part(to_slot, h), bank_send.at[n], bank_sem.at[to_slot, h], device(**to))

    def forward_cap(slot, t):
        if slot in (1, 2):
            send_cap(slot, t, slot + 1, 1)
        elif slot == 3 and t == 0:
            send_cap(3, 0, 7, 1)
        elif slot in (4, 5):
            send_cap(slot, t, slot + 1, -1)
        elif slot == 6 and t == 1:
            send_cap(6, 1, 7, -1)

    def forward_bank(slot, h):
        if slot == 1 and h == 0:
            send_bank(1, 0, 3, dy=1)
        if slot == 2 and h == 1:
            send_bank(2, 1, 3, dy=-1)
        if slot < 4:
            send_bank(slot, h, slot + 4, flip=1)

    def arrived(ref, sem):
        pltpu.make_async_copy(ref, ref, sem).wait()

    def body(*accs):
        accs = (accs[:4], accs[4:])
        own = []
        for t in range(2):
            own.append(pltpu.make_async_copy(caps_hbm.at[pl.ds(t * TILE, TILE), :], cap_part(0, t), local_sem.at[t]))
        for h in range(2):
            own.append(pltpu.make_async_copy(bank_hbm.at[pl.ds(h * HALF, HALF), :], bank_part(0, h), local_sem.at[2 + h]))
        for copy in own:
            copy.start()

        barrier = pltpu.get_barrier_semaphore()
        neighbours = [
            device(flip=1), device(dz=1), device(dz=-1), device(dy=1), device(dy=-1), device(dx=1), device(dx=NX - 1),
        ]
        for neighbour in neighbours:
            pl.semaphore_signal(barrier, inc=1, device_id=neighbour, device_id_type=MESH)

        nothing = jnp.zeros((ROWS, 2 * E), jnp.bfloat16)
        for m in range(2):
            pltpu.matmul_acc_lhs(accs[m][3], nothing, load_staged_rhs=0)
        for m in range(2):
            for acc in accs[m]:
                pltpu.matmul_pop(acc)

        pl.semaphore_wait(barrier, len(neighbours))
        for t in range(2):
            own[t].wait()
        send_cap(0, 0, 1, 1)
        send_cap(0, 1, 4, -1)
        send_cap(0, 1, 1, 1)
        send_cap(0, 0, 4, -1)
        for h in range(2):
            own[2 + h].wait()
            send_bank(0, h, 4, flip=1)
            send_bank(0, h, 1, dy=1)
            send_bank(0, h, 2, dy=-1)

        lane = lax.broadcasted_iota(jnp.int32, (8, 128), 1) % K

        def finish(g):
            found = peaks[g].reshape(8, 2, 8, COLS)
            found = jnp.max(jnp.maximum(found[:, 0], found[:, 1]), axis=1)
            for b in range(8):
                rows[pl.ds(row_of[b], 1), :] = found[b : b + 1, :]
            whole = None
            for q in range(4):
                part = rows[:, q * 128 : (q + 1) * 128]
                for shift in (1, 2, 4):
                    part = jnp.maximum(part, pltpu.roll(part, 128 - shift, 1))
                if q:
                    part = pltpu.roll(part, q, 1)
                whole = part if whole is None else jnp.where(lane == q, part, whole)
            tiles[g] = whole
            if g == 0:
                table[here] = whole
            for dx in range(NX):
                if g == 0 and dx == 0:
                    continue
                n = counts["t"]
                counts["t"] += 1
                send(tiles.at[g], table.at[here], tile_send.at[n], tile_sem.at[here], device(dx=dx, dz=DZ[g]))

        order = program()
        units = [o[1:] for o in order if o[0] == "u"]
        state = {"n": 0, "loaded": None}
        pending = []
        partial = [None, None]
        left = [32] * 8

        def pop_one():
            (g, b, h), c, slot = pending.pop(0)
            for m in range(2):
                value = jnp.max(pltpu.matmul_pop(accs[m][slot]).reshape(ROWS // 8, 8, 2 * E), axis=0)
                if c == 0:
                    partial[m] = value
                else:
                    peaks[g, 2 * b + h, :, m * TILE : (m + 1) * TILE] = jnp.maximum(partial[m], value)
            left[g] -= 1
            if left[g] == 0:
                finish(g)

        def push(g):
            for m in range(2):
                pltpu.matmul_push_rhs(
                    widened(caps[g, m * TILE : (m + 1) * TILE, :]), staging_register=0, mxu_index=m, transpose=True
                )

        present = {0}
        at = 0
        for step in order:
            if step[0] == "c":
                _, slot, t = step
                arrived(cap_part(slot, t), cap_sem.at[slot, t])
                forward_cap(slot, t)
                continue
            if step[0] == "b":
                _, slot, h = step
                arrived(bank_part(slot, h), bank_sem.at[slot, h])
                forward_bank(slot, h)
                continue
            if step[0] == "ready1":
                for dx in (1, NX - 1):
                    pl.semaphore_signal(ready_a, inc=1, device_id=device(dx=dx), device_id_type=MESH)
                continue
            if step[0] == "ready2":
                pl.semaphore_wait(ready_a, 2)
                pl.semaphore_signal(ready_b, inc=1, device_id=device(dx=1), device_id_type=MESH)
                continue
            if step[0] == "ready3":
                pl.semaphore_wait(ready_b, 1)
                continue
            g, b, h = step[1:]
            for c in range(HALF // ROWS):
                first = h * HALF + c * ROWS
                lhs = widened(bank[b, first : first + ROWS, :])
                slot = state["n"] % 4
                state["n"] += 1
                fresh = state["loaded"] != g
                if fresh:
                    push(g)
                    state["loaded"] = g
                for m in range(2):
                    pltpu.matmul_acc_lhs(accs[m][slot], lhs, load_staged_rhs=0 if fresh else None)
                pending.append(((g, b, h), c, slot))
                if len(pending) > 2:
                    pop_one()
        while pending:
            pop_one()

        for dz in range(NZ):
            for dx in range(NX):
                if dx or dz:
                    source = xs[dx] * NZ + zs[dz]
                    arrived(table.at[source], tile_sem.at[source])

        best = jnp.max(jnp.max(table[...], axis=0), axis=0, keepdims=True)
        mine = table[pl.ds(x * NZ, NZ)].reshape(NZ * 8, 128)
        both = jnp.concatenate([mine - best, jnp.broadcast_to(best, (128 - NZ * 8, 128))], axis=0)
        turned[...] = both.T
        by_user = jnp.concatenate([turned[pl.ds(q, USERS // 4, stride=K), :] for q in range(4)], axis=0)
        out_ref[...] = by_user[:, : NZ * 8]
        square = jnp.concatenate([by_user, by_user], axis=0).T
        peak_ref[...] = square[NZ * 8 : NZ * 8 + 8, :]

        for copy in sent:
            copy.wait_send()

    pl.run_scoped(
        body,
        *[pltpu.ACC(0)((ROWS, 2 * E), jnp.float32)] * 4,
        *[pltpu.ACC(1)((ROWS, 2 * E), jnp.float32)] * 4,
    )


def per_device(capsules, bank):
    dma = pltpu.SemaphoreType.DMA
    relative, peak = pl.pallas_call(
        kernel,
        out_shape=(
            jax.ShapeDtypeStruct((USERS, NZ * 8), jnp.float32),
            jax.ShapeDtypeStruct((8, 128), jnp.float32),
        ),
        in_specs=[pl.BlockSpec(memory_space=pltpu.HBM)] * 2,
        out_specs=(pl.BlockSpec(memory_space=pltpu.VMEM),) * 2,
        scratch_shapes=[
            pltpu.VMEM((8, COLS, E), jnp.bfloat16),
            pltpu.VMEM((8, BLOCK, E), jnp.bfloat16),
            pltpu.VMEM((8, 16, 8, COLS), jnp.float32),
            pltpu.VMEM((8, COLS), jnp.float32),
            pltpu.VMEM((8, 8, 128), jnp.float32),
            pltpu.VMEM((NX * NZ, 8, 128), jnp.float32),
            pltpu.VMEM((128, 128), jnp.float32),
            dma((4,)), dma((8, 2)), dma((8, 2)), dma((NX * NZ,)),
            dma((14,)), dma((14,)), dma((31,)),
            pltpu.SemaphoreType.REGULAR, pltpu.SemaphoreType.REGULAR,
        ],
        compiler_params=pltpu.CompilerParams(
            collective_id=0, has_side_effects=True, vmem_limit_bytes=62 << 20
        ),
        name="peaks",
    )(capsules.reshape(COLS, E), bank)
    return relative, peak[0, :USERS]


def solution(mesh):
    return jax.shard_map(
        per_device,
        mesh=mesh,
        in_specs=(P("users", None, None), P(("items", "users"), None)),
        out_specs=(P("users", "items"), P("users")),
        check_vma=False,
    )
```

time: 152 us -> 44.5 us (0.29)
  waiting for transfers between devices: 90.8 us -> 0 us
  Pallas kernels: 0 us -> 40.8 us
  blocking collectives: 22.9 us -> 0 us
  matrix products: 21.6 us -> 0 us
  between operations: 14.1 us -> 0.64 us
    all_gather x1 -> x0, waiting for transfers between devices: 90.1 us -> none  [per_device(): everyone = lax.all_gather(capsules, 'users', axis=0, tiled=True)]
    pallas_call x0 -> x1, Pallas kernels: none -> 40.8 us  [per_device(): pl.pallas_call(kernel, out_shape=(jax.ShapeDtypeStruct((USERS, NZ * 8), j...]
    all_to_all x2 -> x0, blocking collectives: 22.9 us -> none  [the longest x1 15 us: per_device(): lax.all_to_all(own_block, 'users', split_axis=0, concat_axis=1, tiled=True)]
    dot_general x1 -> x0, matrix products: 21.6 us -> none  [one_block(): lax.dot_general(flat, item_rows, (((1,), (1,)), ((), ())), preferred_elem...]
  transfers between devices with their start and end apart: 1 -> 0, of which waited for: 1 -> 0; matrix products, arithmetic and copies ran while one was open for 0% -> 0% of each run, Pallas kernels for 0% -> 0%
where the time goes in v1:
time: 44.5 us; the launch traced here: 44 us
  Pallas kernels  40.8 us (92%)
  local copies, waits for them, and re-layouts  2.57 us (6%)
  between operations  0.64 us (1%)
    pallas_call x1, Pallas kernels, per_device(): pl.pallas_call(kernel, out_shape=(jax.ShapeDtypeStruct((USERS, NZ * 8), j...  40.8 us
    unnamed x1, local copies, waits for them, and re-layouts  1.37 us
    squeeze x1, local copies, waits for them, and re-layouts, per_device(): return (relative, peak[0, :USERS])  1.19 us

profile of v1, /device:TPU:1, one launch (start us, length us, event | category | flops | bytes accessed | tf_op | source)
XLA Modules:
  0.0 44.0 jit_solution(5928544909246674426)
XLA Ops:
  0.6 40.8 %peaks.1 = (f32[64,64]{1,0:T(8,128)}, f32[8,128]{1,0:T(8,128)}) custom-call(bf16[512,128]{1,0:T(8,128)(2,1)} %bitcast.3, bf16[1024,128]{1,0:T(8,128)(2,1)} %bank_hbm.1), custom_call_target="tpu_custom_call" | custom-call | tf_op jit(solution)/shard_map/peaks/pallas_call | solution.py:305
  41.4 1.2 %slice_bitcast_fusion = f32[64]{0:T(128)} fusion(f32[8,128]{1,0:T(8,128)} %get-tuple-element.5), kind=kLoop, calls=%fused_computation | loop fusion | bytes 512 | tf_op jit(solution)/shard_map/squeeze | solution.py:330
  42.6 1.4 %copy.5 = f32[64,64]{1,0:T(8,128)} copy(f32[64,64]{1,0:T(8,128)} %get-tuple-element.8) | data formatting | bytes 32768

commit v2 on v1

v2 whole, which is shorter than its diff:
```python
import jax
import jax.numpy as jnp
from jax import lax
from jax.experimental import pallas as pl
from jax.experimental.pallas import tpu as pltpu
from jax.sharding import PartitionSpec as P

K = 8
E = 128
BLOCK = 1024
USERS = 64
NX, NZ, NY = 4, 8, 4
COLS = USERS * K
TILE = COLS // 2
HALF = BLOCK // 2
ROWS = 256
MESH = pl.DeviceIdType.MESH

DZ = (0, -1, -2, -3, 1, 2, 3, 4)
DY = (0, -1, 1, 2)


def units_of(pairs, blocks):
    return [("u", *pair, b, h) for pair in pairs for b, h in blocks]


def full(*slots):
    return [(b, h) for b in slots for h in (0, 1)]


def half(h, *slots):
    return [(b, h) for b in slots]


def wait_c(*pieces):
    return [("c", s, t) for s, t in pieces]


def wait_b(*pieces):
    return [("b", s, h) for s, h in pieces]


def program():
    own, low, high, opposite = (0, 0), [(1, 4), (2, 5), (3, 6)], [(4, 1), (5, 2), (6, 3)], (7, 7)
    order = []
    order += units_of([own], full(0))
    order += wait_b((4, 0), (4, 1))
    order += units_of([own], full(4))
    order += wait_c((1, 0), (4, 1))
    order += units_of([low[0]], full(0, 4))
    order += wait_c((1, 1), (4, 0))
    order += units_of([high[0]], full(0, 4))
    order += wait_b((1, 0), (2, 0))
    order += units_of([own, low[0], high[0]], half(0, 1, 2))
    order += wait_b((5, 0), (6, 0))
    order += units_of([high[0], low[0]], half(0, 5, 6))
    order += wait_c((2, 0), (5, 1))
    order += units_of([own], half(0, 5, 6))
    order += units_of([low[1]], full(0, 4) + half(0, 1, 2))
    order += wait_c((2, 1), (5, 0)) + wait_b((1, 1), (2, 1))
    order += units_of([low[1]], half(0, 5, 6))
    order += units_of([high[1]], full(0, 4) + half(0, 1, 2, 5, 6))
    order += wait_b((5, 1), (6, 1))
    order += units_of([high[1], low[1]], half(1, 1, 2, 5, 6))
    order += wait_c((3, 0), (6, 1))
    order += units_of([low[0], high[0]], half(1, 1, 2, 5, 6))
    order += units_of([low[2]], full(0, 4))
    order += wait_c((3, 1), (6, 0)) + wait_b((3, 0), (3, 1))
    order += units_of([low[2]], full(1, 2, 5, 6))
    order += wait_b((7, 0), (7, 1))
    order += units_of([high[2]], full(0, 4))
    order += wait_c((7, 0), (7, 1)) + [("ready1",)]
    order += units_of([high[2]], full(1, 2, 5, 6))
    order += units_of([opposite], full(0, 4))
    order += [("ready2",)]
    order += units_of([opposite], full(1, 2, 5, 6))
    order += [("ready3",)]
    order += units_of([(g, g) for g in (4, 5, 6, 7, 3, 2, 1)], full(3, 7))
    order += units_of([own], half(1, 1, 2, 5, 6) + full(3, 7))
    assert len({o for o in order if o[0] == "u"}) == 128
    return order


def widened(value):
    return jnp.concatenate([value, jnp.zeros_like(value)], axis=1)


def kernel(
    caps_hbm, bank_hbm, table,
    caps, bank, peaks, rows, tiles,
    local_sem, cap_sem, bank_sem, tile_sem, send_sem, ready_a, ready_b,
):
    x = lax.axis_index("items")
    u = lax.axis_index("users")
    z = lax.div(u, 2 * NY)
    y = lax.rem(lax.div(u, 2), NY)
    core = lax.rem(u, 2)
    xs = [lax.rem(x + dx, NX) for dx in range(NX)]
    ys = [lax.rem(y + dy, NY) for dy in range(NY)]
    zs = [lax.rem(z + dz, NZ) for dz in range(NZ)]
    here = x * NZ + z
    users_at = {}
    for dz in range(NZ):
        users_at[dz, 0, 0] = (zs[dz] * NY + y) * 2 + core
    for dy in range(1, NY):
        users_at[0, dy, 0] = (z * NY + ys[dy]) * 2 + core
    users_at[0, 0, 1] = (z * NY + y) * 2 + 1 - core
    row_of = [2 * ys[DY[b % 4] % NY] + (core if b < 4 else 1 - core) for b in range(8)]

    def device(dx=0, dz=0, dy=0, flip=0):
        return {"items": xs[dx % NX], "users": users_at[dz % NZ, dy % NY, flip]}

    def cap_part(slot, t):
        return caps.at[slot, pl.ds(t * TILE, TILE), :]

    def bank_part(slot, h):
        return bank.at[slot, pl.ds(h * HALF, HALF), :]

    def send(src, dst, send_sem, recv_sem, to):
        pltpu.make_async_remote_copy(
            src_ref=src, dst_ref=dst, send_sem=send_sem, recv_sem=recv_sem, device_id=to, device_id_type=MESH
        ).start()

    def send_cap(slot, t, to_slot, dz):
        send(cap_part(slot, t), cap_part(to_slot, t), send_sem.at[0], cap_sem.at[to_slot, t], device(dz=dz))

    def send_bank(slot, h, to_slot, **to):
        send(bank_part(slot, h), bank_part(to_slot, h), send_sem.at[1], bank_sem.at[to_slot, h], device(**to))

    def forward_cap(slot, t):
        if slot in (1, 2):
            send_cap(slot, t, slot + 1, 1)
        elif slot == 3 and t == 0:
            send_cap(3, 0, 7, 1)
        elif slot in (4, 5):
            send_cap(slot, t, slot + 1, -1)
        elif slot == 6 and t == 1:
            send_cap(6, 1, 7, -1)

    def forward_bank(slot, h):
        if slot == 1 and h == 0:
            send_bank(1, 0, 3, dy=1)
        if slot == 2 and h == 1:
            send_bank(2, 1, 3, dy=-1)
        if slot < 4:
            send_bank(slot, h, slot + 4, flip=1)

    def arrived(ref, sem):
        pltpu.make_async_copy(ref, ref, sem).wait()

    def body(*accs):
        accs = (accs[:4], accs[4:])
        own = []
        for t in range(2):
            own.append(pltpu.make_async_copy(caps_hbm.at[pl.ds(t * TILE, TILE), :], cap_part(0, t), local_sem.at[t]))
        for h in range(2):
            own.append(pltpu.make_async_copy(bank_hbm.at[pl.ds(h * HALF, HALF), :], bank_part(0, h), local_sem.at[2 + h]))
        for copy in own:
            copy.start()

        barrier = pltpu.get_barrier_semaphore()
        neighbours = [
            device(flip=1), device(dz=1), device(dz=-1), device(dy=1), device(dy=-1), device(dx=1), device(dx=NX - 1),
        ]
        for neighbour in neighbours:
            pl.semaphore_signal(barrier, inc=1, device_id=neighbour, device_id_type=MESH)

        nothing = jnp.zeros((ROWS, 2 * E), jnp.bfloat16)
        for m in range(2):
            pltpu.matmul_acc_lhs(accs[m][3], nothing, load_staged_rhs=0)
        for m in range(2):
            for acc in accs[m]:
                pltpu.matmul_pop(acc)

        pl.semaphore_wait(barrier, len(neighbours))
        for t in range(2):
            own[t].wait()
        send_cap(0, 0, 1, 1)
        send_cap(0, 1, 4, -1)
        send_cap(0, 1, 1, 1)
        send_cap(0, 0, 4, -1)
        for h in range(2):
            own[2 + h].wait()
            send_bank(0, h, 4, flip=1)
            send_bank(0, h, 1, dy=1)
            send_bank(0, h, 2, dy=-1)

        lane = lax.broadcasted_iota(jnp.int32, (8, 128), 1) % K

        def finish(g):
            whole = None
            for q in range(4):
                part = rows[g, :, q * 128 : (q + 1) * 128]
                for shift in (1, 2, 4):
                    part = jnp.maximum(part, pltpu.roll(part, 128 - shift, 1))
                if q:
                    part = pltpu.roll(part, q, 1)
                whole = part if whole is None else jnp.where(lane == q, part, whole)
            tiles[g] = whole
            if g == 0:
                table[here] = whole

        def deliver(g):
            for dx in range(NX):
                if g == 0 and dx == 0:
                    continue
                send(tiles.at[g], table.at[here], send_sem.at[2], tile_sem, device(dx=dx, dz=DZ[g]))

        order = program()
        pending = []
        loaded = [None, None]
        partial = [None, None]
        left = [64] * 8
        begun = set()
        ready = []
        chunks = 0

        def pop_one():
            groups, b, c, slot = pending.pop(0)
            for m in range(2):
                g = groups[m]
                value = jnp.max(pltpu.matmul_pop(accs[m][slot]).reshape(ROWS // 8, 8, 2 * E), axis=0)
                left[g] -= 1
                if c == 0:
                    partial[m] = value
                    continue
                value = jnp.maximum(partial[m], value)
                columns = slice(m * TILE, (m + 1) * TILE)
                if (m, g, b) not in begun:
                    begun.add((m, g, b))
                    peaks[g, b, :, columns] = value
                else:
                    value = jnp.maximum(peaks[g, b, :, columns], value)
                    rows[g, pl.ds(row_of[b], 1), columns] = jnp.max(value, axis=0, keepdims=True)
            for g in sorted(set(groups)):
                if left[g] == 0:
                    finish(g)
                    ready.append([2, g])

        def push(m, g):
            pltpu.matmul_push_rhs(
                widened(caps[g, m * TILE : (m + 1) * TILE, :]), staging_register=0, mxu_index=m, transpose=True
            )

        for step in order:
            if step[0] == "c":
                _, slot, t = step
                arrived(cap_part(slot, t), cap_sem.at[slot, t])
                forward_cap(slot, t)
                continue
            if step[0] == "b":
                _, slot, h = step
                arrived(bank_part(slot, h), bank_sem.at[slot, h])
                forward_bank(slot, h)
                continue
            if step[0] == "ready1":
                for dx in (1, NX - 1):
                    pl.semaphore_signal(ready_a, inc=1, device_id=device(dx=dx), device_id_type=MESH)
                continue
            if step[0] == "ready2":
                pl.semaphore_wait(ready_a, 2)
                pl.semaphore_signal(ready_b, inc=1, device_id=device(dx=1), device_id_type=MESH)
                continue
            if step[0] == "ready3":
                pl.semaphore_wait(ready_b, 1)
                continue
            for item in ready:
                item[0] -= 1
            while ready and ready[0][0] < 0:
                deliver(ready.pop(0)[1])
            groups, b, h = step[1:3], step[3], step[4]
            for c in range(HALF // ROWS):
                first = h * HALF + c * ROWS
                lhs = widened(bank[b, first : first + ROWS, :])
                slot = chunks % 4
                chunks += 1
                for m in range(2):
                    fresh = loaded[m] != groups[m]
                    if fresh:
                        push(m, groups[m])
                        loaded[m] = groups[m]
                    pltpu.matmul_acc_lhs(accs[m][slot], lhs, load_staged_rhs=0 if fresh else None)
                pending.append((groups, b, c, slot))
                if len(pending) > 2:
                    pop_one()
        while pending:
            pop_one()
        while ready:
            deliver(ready.pop(0)[1])

        arrived(table.at[pl.ds(0, NX * NZ - 1)], tile_sem)
        arrived(caps.at[pl.ds(0, 7)], send_sem.at[0])
        arrived(bank.at[pl.ds(0, 7)], send_sem.at[1])
        arrived(table.at[pl.ds(0, NX * NZ - 1)], send_sem.at[2])

    pl.run_scoped(
        body,
        *[pltpu.ACC(0)((ROWS, 2 * E), jnp.float32)] * 4,
        *[pltpu.ACC(1)((ROWS, 2 * E), jnp.float32)] * 4,
    )


def ending(table, out_ref, peak_ref, turned):
    x = lax.axis_index("items")
    best = jnp.max(jnp.max(table[...], axis=0), axis=0, keepdims=True)
    mine = table[pl.ds(x * NZ, NZ)].reshape(NZ * 8, 128)
    both = jnp.concatenate([mine - best, jnp.broadcast_to(best, (128 - NZ * 8, 128))], axis=0)
    turned[...] = both.T
    by_user = jnp.concatenate([turned[pl.ds(q, USERS // 4, stride=K), :] for q in range(4)], axis=0)
    out_ref[...] = by_user[:, : NZ * 8]
    square = jnp.concatenate([by_user, by_user], axis=0).T
    peak_ref[...] = square[NZ * 8, :USERS]


def per_device(capsules, bank):
    dma = pltpu.SemaphoreType.DMA
    vmem = pl.BlockSpec(memory_space=pltpu.VMEM)
    table = pl.pallas_call(
        kernel,
        out_shape=jax.ShapeDtypeStruct((NX * NZ, 8, 128), jnp.float32),
        in_specs=[pl.BlockSpec(memory_space=pltpu.HBM)] * 2,
        out_specs=vmem,
        scratch_shapes=[
            pltpu.VMEM((8, COLS, E), jnp.bfloat16),
            pltpu.VMEM((8, BLOCK, E), jnp.bfloat16),
            pltpu.VMEM((8, 8, 8, COLS), jnp.float32),
            pltpu.VMEM((8, 8, COLS), jnp.float32),
            pltpu.VMEM((8, 8, 128), jnp.float32),
            dma((4,)), dma((8, 2)), dma((8, 2)), dma, dma((3,)),
            pltpu.SemaphoreType.REGULAR, pltpu.SemaphoreType.REGULAR,
        ],
        compiler_params=pltpu.CompilerParams(
            collective_id=0, has_side_effects=True, vmem_limit_bytes=40 << 20
        ),
        name="peaks",
    )(
        pltpu.with_memory_space_constraint(capsules.reshape(COLS, E), pltpu.HBM),
        pltpu.with_memory_space_constraint(bank, pltpu.HBM),
    )
    return pl.pallas_call(
        ending,
        out_shape=(
            jax.ShapeDtypeStruct((USERS, NZ * 8), jnp.float32),
            jax.ShapeDtypeStruct((USERS,), jnp.float32),
        ),
        in_specs=[vmem],
        out_specs=(vmem, vmem),
        scratch_shapes=[pltpu.VMEM((128, 128), jnp.float32)],
        compiler_params=pltpu.CompilerParams(vmem_limit_bytes=4 << 20),
        name="ending",
    )(table)


def solution(mesh):
    return jax.shard_map(
        per_device,
        mesh=mesh,
        in_specs=(P("users", None, None), P(("items", "users"), None)),
        out_specs=(P("users", "items"), P("users")),
        check_vma=False,
    )
```

time: 44.5 us -> 39 us (0.88)
  local copies, waits for them, and re-layouts: 2.57 us -> 0 us
  Pallas kernels: 40.8 us -> 38.3 us
    pallas_call x1 -> x2, Pallas kernels: 40.8 us -> 38.3 us  [the longest x1 37.5 us: per_device(): pl.pallas_call(kernel, out_shape=jax.ShapeDtypeStruct((NX * NZ, 8, 128),...]
    unnamed x1 -> x0, local copies, waits for them, and re-layouts: 1.37 us -> none
    squeeze x1 -> x0, local copies, waits for them, and re-layouts: 1.19 us -> none  [per_device(): return (relative, peak[0, :USERS])]
where the time goes in v2:
time: 39 us; the launch traced here: 38.9 us
  Pallas kernels  38.3 us (98%)
  between operations  0.64 us (2%)
    pallas_call x1, Pallas kernels, per_device(): pl.pallas_call(kernel, out_shape=jax.ShapeDtypeStruct((NX * NZ, 8, 128),...  37.5 us

profile of v2, /device:TPU:1, one launch (start us, length us, event | category | flops | bytes accessed | tf_op | source)
XLA Modules:
  0.0 38.9 jit_solution(8834421412743236035)
XLA Ops:
  0.6 37.5 %peaks.1.table = f32[32,8,128]{2,1,0:T(8,128)S(1)} custom-call(bf16[512,128]{1,0:T(8,128)(2,1)} %bitcast.1, bf16[1024,128]{1,0:T(8,128)(2,1)} %bank_hbm.1), custom_call_target="tpu_custom_call" | custom-call | tf_op jit(solution)/shard_map/peaks/pallas_call | solution.py:318
  38.2 0.7 %ending.1 = (f32[64,64]{1,0:T(8,128)}, f32[64]{0:T(128)}) custom-call(f32[32,8,128]{2,1,0:T(8,128)S(1)} %peaks.1.table), custom_call_target="tpu_custom_call" | custom-call | tf_op jit(solution)/shard_map/ending/pallas_call | solution.py:340

commit v3 on v2

--- a/solution.py
+++ b/solution.py
@@ -61,20 +61,20 @@
     order += units_of([low[1]], half(0, 5, 6))
     order += units_of([high[1]], full(0, 4) + half(0, 1, 2, 5, 6))
     order += wait_b((5, 1), (6, 1))
-    order += units_of([high[1], low[1]], half(1, 1, 2, 5, 6))
+    order += units_of([high[1], low[1], low[0]], half(1, 1, 2, 5, 6))
     order += wait_c((3, 0), (6, 1))
-    order += units_of([low[0], high[0]], half(1, 1, 2, 5, 6))
+    order += units_of([high[0]], half(1, 1, 2, 5, 6))
+    order += wait_b((3, 0), (3, 1))
     order += units_of([low[2]], full(0, 4))
-    order += wait_c((3, 1), (6, 0)) + wait_b((3, 0), (3, 1))
+    order += wait_c((3, 1), (6, 0)) + [("ready1",)]
     order += units_of([low[2]], full(1, 2, 5, 6))
     order += wait_b((7, 0), (7, 1))
-    order += units_of([high[2]], full(0, 4))
-    order += wait_c((7, 0), (7, 1)) + [("ready1",)]
-    order += units_of([high[2]], full(1, 2, 5, 6))
-    order += units_of([opposite], full(0, 4))
-    order += [("ready2",)]
-    order += units_of([opposite], full(1, 2, 5, 6))
+    order += units_of([high[2]], full(0, 4, 1, 2))
+    order += [("ready2",)] + wait_c((7, 0), (7, 1))
+    order += units_of([high[2]], full(5, 6))
+    order += units_of([opposite], full(0, 4, 1, 2))
     order += [("ready3",)]
+    order += units_of([opposite], full(5, 6))
     order += units_of([(g, g) for g in (4, 5, 6, 7, 3, 2, 1)], full(3, 7))
     order += units_of([own], half(1, 1, 2, 5, 6) + full(3, 7))
     assert len({o for o in order if o[0] == "u"}) == 128

time: 39 us -> 38.4 us (0.985)
  Pallas kernels: 38.3 us -> 37.7 us
    pallas_call x1, Pallas kernels: 37.5 us -> 37 us  [per_device(): pl.pallas_call(kernel, out_shape=jax.ShapeDtypeStruct((NX * NZ, 8, 128),...]
where the time goes in v3:
time: 38.4 us; the launch traced here: 38.3 us
  Pallas kernels  37.7 us (98%)
  between operations  0.64 us (2%)
    pallas_call x1, Pallas kernels, per_device(): pl.pallas_call(kernel, out_shape=jax.ShapeDtypeStruct((NX * NZ, 8, 128),...  37 us

profile of v3, /device:TPU:1, one launch (start us, length us, event | category | flops | bytes accessed | tf_op | source)
XLA Modules:
  0.0 38.3 jit_solution(4710896910239734401)
XLA Ops:
  0.6 37.0 %peaks.1.table = f32[32,8,128]{2,1,0:T(8,128)S(1)} custom-call(bf16[512,128]{1,0:T(8,128)(2,1)} %bitcast.1, bf16[1024,128]{1,0:T(8,128)(2,1)} %bank_hbm.1), custom_call_target="tpu_custom_call" | custom-call | tf_op jit(solution)/shard_map/peaks/pallas_call | solution.py:318
  37.6 0.7 %ending.1 = (f32[64,64]{1,0:T(8,128)}, f32[64]{0:T(128)}) custom-call(f32[32,8,128]{2,1,0:T(8,128)S(1)} %peaks.1.table), custom_call_target="tpu_custom_call" | custom-call | tf_op jit(solution)/shard_map/ending/pallas_call | solution.py:340

commit v4 on v3

--- a/solution.py
+++ b/solution.py
@@ -75,7 +75,7 @@
     order += units_of([opposite], full(0, 4, 1, 2))
     order += [("ready3",)]
     order += units_of([opposite], full(5, 6))
-    order += units_of([(g, g) for g in (4, 5, 6, 7, 3, 2, 1)], full(3, 7))
+    order += units_of([(g, g) for g in (7, 6, 5, 4, 3, 2, 1)], full(3, 7))
     order += units_of([own], half(1, 1, 2, 5, 6) + full(3, 7))
     assert len({o for o in order if o[0] == "u"}) == 128
     return order
@@ -201,7 +201,7 @@
                 table[here] = whole
 
         def deliver(g):
-            for dx in range(NX):
+            for dx in (2, 1, 3, 0):
                 if g == 0 and dx == 0:
                     continue
                 send(tiles.at[g], table.at[here], send_sem.at[2], tile_sem, device(dx=dx, dz=DZ[g]))

time: 38.4 us -> 38.2 us (level)
  no operation moved by 1% of the time
where the time goes in v4:
time: 38.2 us; the launch traced here: 38.1 us
  Pallas kernels  37.5 us (98%)
  between operations  0.64 us (2%)
    pallas_call x1, Pallas kernels, per_device(): pl.pallas_call(kernel, out_shape=jax.ShapeDtypeStruct((NX * NZ, 8, 128),...  36.8 us

profile of v4, /device:TPU:1, one launch (start us, length us, event | category | flops | bytes accessed | tf_op | source)
XLA Modules:
  0.0 38.1 jit_solution(12157321156529044826)
XLA Ops:
  0.6 36.8 %peaks.1.table = f32[32,8,128]{2,1,0:T(8,128)S(1)} custom-call(bf16[512,128]{1,0:T(8,128)(2,1)} %bitcast.1, bf16[1024,128]{1,0:T(8,128)(2,1)} %bank_hbm.1), custom_call_target="tpu_custom_call" | custom-call | tf_op jit(solution)/shard_map/peaks/pallas_call | solution.py:318
  37.4 0.7 %ending.1 = (f32[64,64]{1,0:T(8,128)}, f32[64]{0:T(128)}) custom-call(f32[32,8,128]{2,1,0:T(8,128)S(1)} %peaks.1.table), custom_call_target="tpu_custom_call" | custom-call | tf_op jit(solution)/shard_map/ending/pallas_call | solution.py:340

commit v5 on v4

--- a/solution.py
+++ b/solution.py
@@ -55,7 +55,6 @@
     order += wait_b((5, 0), (6, 0))
     order += units_of([high[0], low[0]], half(0, 5, 6))
     order += wait_c((2, 0), (5, 1))
-    order += units_of([own], half(0, 5, 6))
     order += units_of([low[1]], full(0, 4) + half(0, 1, 2))
     order += wait_c((2, 1), (5, 0)) + wait_b((1, 1), (2, 1))
     order += units_of([low[1]], half(0, 5, 6))
@@ -76,7 +75,7 @@
     order += [("ready3",)]
     order += units_of([opposite], full(5, 6))
     order += units_of([(g, g) for g in (7, 6, 5, 4, 3, 2, 1)], full(3, 7))
-    order += units_of([own], half(1, 1, 2, 5, 6) + full(3, 7))
+    order += units_of([own], half(0, 5, 6) + half(1, 1, 2, 5, 6) + full(3, 7))
     assert len({o for o in order if o[0] == "u"}) == 128
     return order
 

time: 38.2 us -> 38.1 us (level)
  no operation moved by 1% of the time
where the time goes in v5:
time: 38.1 us; the launch traced here: 37.9 us
  Pallas kernels  37.3 us (98%)
  between operations  0.64 us (2%)
    pallas_call x1, Pallas kernels, per_device(): pl.pallas_call(kernel, out_shape=jax.ShapeDtypeStruct((NX * NZ, 8, 128),...  36.5 us

profile of v5, /device:TPU:1, one launch (start us, length us, event | category | flops | bytes accessed | tf_op | source)
XLA Modules:
  0.0 37.9 jit_solution(16107617834584541122)
XLA Ops:
  0.6 36.5 %peaks.1.table = f32[32,8,128]{2,1,0:T(8,128)S(1)} custom-call(bf16[512,128]{1,0:T(8,128)(2,1)} %bitcast.1, bf16[1024,128]{1,0:T(8,128)(2,1)} %bank_hbm.1), custom_call_target="tpu_custom_call" | custom-call | tf_op jit(solution)/shard_map/peaks/pallas_call | solution.py:317
  37.2 0.7 %ending.1 = (f32[64,64]{1,0:T(8,128)}, f32[64]{0:T(128)}) custom-call(f32[32,8,128]{2,1,0:T(8,128)S(1)} %peaks.1.table), custom_call_target="tpu_custom_call" | custom-call | tf_op jit(solution)/shard_map/ending/pallas_call | solution.py:339
